TPU v7x, 32 devices: a whole 2x2x4 slice. The times are simulated.
32 devices in a mesh: io: 16 (over z, x, core), rep: 2 (over y).
Axes of the slice: x: 2, y: 2, z: 4, core: 2. Of those that a mesh axis runs over, the one named last changes fastest.
Arguments:
- snapshots: float32 [49152, 2048], P(('rep', 'io')), parts along dimension 0, may hold values from -6 to 6
Outputs:
- coefficients: float32 [32, 256, 2048], P('rep', None, 'io'), parts along dimension 0
- resid_var: float32 [512, 2048], P('rep', 'io'), parts along dimension 0
There are 2 independent parts, one for each index of `rep`. A program takes and returns all parts, laid end to end along the dimension named above; each array names one. Nothing has to cross between parts.
All inputs are finite; a program needn't handle non-finite values.
Results may differ from a plain program's by a relative error of at most 0.000071.
Values sent between devices are 32-bit elements; how exact they have to be, the bound alone decides.
A program may use at most 128 MiB of HBM per device.

v0:
```python
import jax
import jax.numpy as jnp
from jax import lax
from jax.sharding import PartitionSpec as P

TIMES = 96
HARM = 16


def basis_matrix(times):
    steps = jnp.arange(times).astype(jnp.float32)
    columns = [jnp.ones_like(steps), (steps - (times - 1) / 2.0) / (times / 2.0)]
    for harmonic in range(1, 7):
        columns.append(jnp.cos(2.0 * jnp.pi * harmonic * steps / 12.0))
    for harmonic in range(1, 6):
        columns.append(jnp.sin(2.0 * jnp.pi * harmonic * steps / 12.0))
    columns.append(jnp.cos(2.0 * jnp.pi * steps / times))
    columns.append(jnp.sin(2.0 * jnp.pi * steps / times))
    columns.append(jnp.cos(4.0 * jnp.pi * steps / times))
    return jnp.stack(columns, axis=1)


def projector_of(basis):
    gram = jnp.dot(basis.T, basis, precision=lax.Precision.HIGHEST)
    factor = jnp.linalg.cholesky(gram)
    middle = lax.linalg.triangular_solve(factor, basis.T, left_side=True, lower=True)
    return lax.linalg.triangular_solve(factor, middle, left_side=True, lower=True, transpose_a=True)


def fit_block(block, basis, projector):
    width = block.shape[-1]
    lat_rows = block.shape[0] // TIMES
    series = block.reshape(TIMES, lat_rows * width)
    coeffs = jnp.dot(projector, series, precision=lax.Precision.HIGHEST)
    moments = jnp.dot(basis.T, series, precision=lax.Precision.HIGHEST)
    total = jnp.sum(series * series, axis=0)
    variance = (total - jnp.sum(coeffs * moments, axis=0)) / TIMES
    return (coeffs.reshape(HARM, lat_rows, width), variance.reshape(1, lat_rows, width))


def local(snapshots):
    groups = lax.axis_size("io")
    local_rows = snapshots.shape[0]
    lon_dev = snapshots.shape[1] // groups
    split_view = snapshots.reshape(local_rows, groups, lon_dev)
    basis = basis_matrix(TIMES)
    projector = projector_of(basis)
    moved = lax.all_to_all(split_view, "io", split_axis=1, concat_axis=0, tiled=True)
    coeffs, variance = fit_block(moved[:, 0, :], basis, projector)
    return (coeffs, variance[0])


def solution(mesh):
    placed = (P(("rep", "io"), None),)
    return jax.shard_map(
        local,
        mesh=mesh,
        in_specs=placed,
        out_specs=(P("rep", None, "io"), P("rep", "io")),
        check_vma=False,
    )
```

profile of v0, /device:TPU:11, one launch (start us, length us, event | category | flops | bytes accessed | tf_op | source)
XLA Modules:
  0.0 326.1 jit_solution(2681641074615959106)
XLA Ops:
  0.6 10.3 %copy_bitcast_fusion = f32[1536,16,128]{2,0,1:T(8,128)} fusion(f32[1536,2048]{1,0:T(8,128)} %param.1), kind=kLoop, calls=%fused_computation.1 | loop fusion | bytes 25165824 | tf_op jit(solution)/shard_map/reshape | solution.py:45
  10.9 6.5 %all-to-all-start = ((f32[1536,16,128]{2,0,1:T(8,128)}), f32[1536,16,128]{2,0,1:T(8,128)}, u32[]{:S(2)}, u32[]{:S(2)}) async-start(f32[1536,16,128]{2,0,1:T(8,128)} %copy_bitcast_fusion), calls=%async_computation | async-start | bytes 25165824 | tf_op jit(solution)/shard_map/all_to_all | solution.py:48
  17.5 0.1 fusion.16
  17.6 0.1 fusion.14
  17.6 0.1 fusion.12
  17.7 0.1 fusion.10
  17.7 0.1 fusion.8
  17.8 0.1 multiply_cosine_fusion
  17.9 0.1 stack.2
  18.0 0.1 fusion.19
  18.1 0.1 copy.6
  18.2 1.5 cholesky.16
  19.7 0.6 compare_reduce_fusion
  20.3 0.6 fusion.1
  21.0 1.2 custom-call.8
  22.2 0.2 fusion.4
  22.4 0.1 fusion.2
  22.5 267.2 %all-to-all-done = f32[1536,16,128]{2,0,1:T(8,128)} async-done(((f32[1536,16,128]{2,0,1:T(8,128)}), f32[1536,16,128]{2,0,1:T(8,128)}, u32[]{:S(2)}, u32[]{:S(2)}) %all-to-all-start) | async-done | bytes 12582944 | tf_op jit(solution)/shard_map/all_to_all | solution.py:48
  289.7 13.8 %reshape_squeeze.3 = f32[96,32768]{1,0:T(8,128)} reshape(f32[16,1536,1,128]{3,1,0,2:T(8,128)} %bitcast.4) | data formatting | bytes 25165824 | tf_op jit(solution)/shard_map/reshape;squeeze | solution.py:33
  303.5 0.0 copy-start
  303.5 5.8 %multiply_reduce_fusion = f32[32768]{0:T(1024)S(1)} fusion(f32[96,32768]{1,0:T(8,128)} %reshape_squeeze.3), kind=kLoop, calls=%fused_computation.2 | loop fusion | flops 6258688 | bytes 12713984 | tf_op jit(solution)/shard_map/reduce_sum | solution.py:36
  309.3 2.4 copy-done
  311.7 6.0 %fusion.20 = f32[16,32768]{1,0:T(8,128)S(1)} fusion(f32[16,96]{1,0:T(8,128)S(1)} %fusion.2, f32[96,32768]{1,0:T(8,128)S(1)} %copy-done), kind=kOutput, calls=%fused_computation.39 | convolution fusion | flops 603979776 | bytes 14686208 | tf_op jit(solution)/shard_map/dot_general | solution.py:34
  317.6 6.1 %fusion = f32[32768]{0:T(1024)S(1)} fusion(f32[16,32768]{1,0:T(8,128)S(1)} %fusion.20, f32[96,16]{0,1:T(8,128)S(1)} %stack.2, f32[96,32768]{1,0:T(8,128)S(1)} %copy-done), kind=kOutput, calls=%fused_computation.3 | convolution fusion | flops 604995584 | bytes 14817280 | tf_op jit(solution)/shard_map/dot_general | solution.py:35
  323.7 1.7 copy.9
  325.4 0.7 multiply_bitcast_fusion
  (5 shorter events, 0.1 us)
Async XLA Ops:
  10.9 278.8 %all-to-all-start = ((f32[1536,16,128]{2,0,1:T(8,128)}), f32[1536,16,128]{2,0,1:T(8,128)}, u32[]{:S(2)}, u32[]{:S(2)}) async-start(f32[1536,16,128]{2,0,1:T(8,128)} %copy_bitcast_fusion), calls=%async_computation | async-start | bytes 25165824 | tf_op jit(solution)/shard_map/all_to_all | solution.py:48
  303.5 8.2 %copy-start = (f32[96,32768]{1,0:T(8,128)S(1)}, f32[96,32768]{1,0:T(8,128)}, u32[]{:S(2)}) copy-start(f32[96,32768]{1,0:T(8,128)} %reshape_squeeze.3) | copy-start | bytes 37748740
where the time goes:
time: 327 us; the launch traced here: 326 us
  waiting for transfers between devices  267 us (82%)
  local copies, waits for them, and re-layouts  28.3 us (9%)
  matrix products  12.5 us (4%)
  other arithmetic  10.9 us (3%)
  starting transfers between devices  6.52 us (2%)
    all_to_all x1, waiting for transfers between devices, local(): lax.all_to_all(split_view, 'io', split_axis=1, concat_axis=0, tiled=True)  267 us
    another operation x1, local copies, waits for them, and re-layouts, fit_block(): series = block.reshape(TIMES, lat_rows * width)  13.8 us
    reshape x1, local copies, waits for them, and re-layouts, local(): split_view = snapshots.reshape(local_rows, groups, lon_dev)  10.3 us
  transfers between devices with their start and end apart: 1, of which 1 were waited for; matrix products, arithmetic and copies ran while one was open for 2% of the time, Pallas kernels for 0%

commit v1 on v0

--- a/solution.py
+++ b/solution.py
@@ -45,7 +45,10 @@
     split_view = snapshots.reshape(local_rows, groups, lon_dev)
     basis = basis_matrix(TIMES)
     projector = projector_of(basis)
-    moved = lax.all_to_all(split_view, "io", split_axis=1, concat_axis=0, tiled=True)
+    moved = jnp.concatenate(
+        lax.all_to_all(jnp.stack(jnp.split(split_view, lax.axis_size("io"), axis=1)), "io", 0, 0),
+        axis=0,
+    )
     coeffs, variance = fit_block(moved[:, 0, :], basis, projector)
     return (coeffs, variance[0])
 

time: 327 us -> 392 us (1.20)
  local copies, waits for them, and re-layouts: 28.3 us -> 93.7 us
    split x0 -> x1, local copies, waits for them, and re-layouts: none -> 39.1 us  [local(): jnp.split(split_view, lax.axis_size('io'), axis=1)]
    unnamed x3 -> x27, local copies, waits for them, and re-layouts: 4.09 us -> 39.7 us
    reshape x1 -> x0, local copies, waits for them, and re-layouts: 10.3 us -> none  [local(): split_view = snapshots.reshape(local_rows, groups, lon_dev)]
  transfers between devices with their start and end apart: 1 -> 1, of which waited for: 1 -> 1; matrix products, arithmetic and copies ran while one was open for 2% -> 1% of each run, Pallas kernels for 0% -> 0%
where the time goes in v1:
time: 392 us
  waiting for transfers between devices  267 us (68%)
  local copies, waits for them, and re-layouts  93.7 us (24%)
  matrix products  12.5 us (3%)
  other arithmetic  10.9 us (3%)
  starting transfers between devices  6.52 us (2%)
    all_to_all x1, waiting for transfers between devices, local(): lax.all_to_all(jnp.stack(jnp.split(split_view, lax.axis_size('io'), axis=...  267 us
    unnamed x27, local copies, waits for them, and re-layouts  39.7 us
    split x1, local copies, waits for them, and re-layouts, local(): jnp.split(split_view, lax.axis_size('io'), axis=1)  39.1 us
    another operation x1, local copies, waits for them, and re-layouts, fit_block(): series = block.reshape(TIMES, lat_rows * width)  13.8 us
  transfers between devices with their start and end apart: 1, of which 1 were waited for; matrix products, arithmetic and copies ran while one was open for 1% of the time, Pallas kernels for 0%

profile of v1, /device:TPU:11, one launch (start us, length us, event | category | flops | bytes accessed | tf_op | source)
XLA Modules:
  0.0 391.5 jit_solution(15239439849811728294)
XLA Ops:
  0.6 12.2 %copy.50 = f32[192,8,16,128]{3,2,1,0:T(8,128)} copy(f32[192,8,16,128]{3,1,2,0:T(8,128)} %bitcast.77) | data formatting | bytes 25165824
  12.8 39.1 %fusion.19 = (f32[1536,1,128]{2,1,0:T(1,128)S(1)}, f32[1536,1,128]{2,1,0:T(1,128)S(1)}, f32[1536,1,128]{2,1,0:T(1,128)S(1)}, f32[1536,1,128]{2,1,0:T(1,128)}, f3...) fusion(f32[1536,16,128]{2,1,0:T(8,128)} %bitcast.75), kind=kLoop, calls=%fused_computation.53 | loop fusion | bytes 25165824 | tf_op jit(solution)/shard_map/split | solution.py:49
  52.0 2.2 constant_dynamic-update-slice_fusion.15
  54.2 2.1 constant_dynamic-update-slice_fusion.14
  56.3 2.1 constant_dynamic-update-slice_fusion.13
  58.3 2.1 constant_dynamic-update-slice_fusion.12
  60.4 2.1 constant_dynamic-update-slice_fusion.11
  62.5 2.1 constant_dynamic-update-slice_fusion.10
  64.5 2.1 constant_dynamic-update-slice_fusion.9
  66.6 2.1 constant_dynamic-update-slice_fusion.8
  68.7 0.9 constant_dynamic-update-slice_fusion.7
  69.6 0.9 constant_dynamic-update-slice_fusion.6
  70.6 1.0 constant_dynamic-update-slice_fusion.5
  71.6 1.0 constant_dynamic-update-slice_fusion.4
  72.6 0.9 constant_dynamic-update-slice_fusion.3
  73.5 1.0 constant_dynamic-update-slice_fusion.2
  74.5 0.9 constant_dynamic-update-slice_fusion.1
  75.4 1.0 constant_dynamic-update-slice_fusion
  76.4 6.5 %all-to-all-start = ((f32[16,1536,1,128]{3,1,2,0:T(8,128)}), f32[16,1536,1,128]{3,1,2,0:T(8,128)}, u32[]{:S(2)}, u32[]{:S(2)}) async-start(f32[16,1536,1,128]{3,1,2,0:T(8,128)} %constant_dynamic-update-slice_fusion), calls=%async_computation | async-start | bytes 25165824 | tf_op jit(solution)/shard_map/all_to_all | solution.py:49
  83.6 1.5 cholesky.16
  85.1 0.6 compare_reduce_fusion
  85.7 0.6 fusion.1
  86.4 1.2 custom-call.8
  87.6 0.2 fusion.4
  88.0 267.2 %all-to-all-done = f32[16,1536,1,128]{3,1,2,0:T(8,128)} async-done(((f32[16,1536,1,128]{3,1,2,0:T(8,128)}), f32[16,1536,1,128]{3,1,2,0:T(8,128)}, u32[]{:S(2)}, u32[]{:S(2)}) %all-to-all-start) | async-done | bytes 12582944 | tf_op jit(solution)/shard_map/all_to_all | solution.py:49
  355.1 13.8 %reshape_squeeze_reshape.3 = f32[96,32768]{1,0:T(8,128)} reshape(f32[16,1536,1,128]{3,1,2,0:T(8,128)} %all-to-all-done) | data formatting | bytes 25165824 | tf_op jit(solution)/shard_map/reshape;squeeze;reshape | solution.py:33
  368.9 5.8 %multiply_reduce_fusion = f32[32768]{0:T(1024)S(1)} fusion(f32[96,32768]{1,0:T(8,128)} %reshape_squeeze_reshape.3), kind=kLoop, calls=%fused_computation.1 | loop fusion | flops 6258688 | bytes 12713984 | tf_op jit(solution)/shard_map/reduce_sum | solution.py:36
  374.7 2.4 copy-done
  377.1 6.0 %fusion.21 = f32[16,32768]{1,0:T(8,128)S(1)} fusion(f32[16,96]{1,0:T(8,128)S(1)} %fusion.2, f32[96,32768]{1,0:T(8,128)S(1)} %copy-done), kind=kOutput, calls=%fused_computation.55 | convolution fusion | flops 603979776 | bytes 14686208 | tf_op jit(solution)/shard_map/dot_general | solution.py:34
  383.0 6.1 %fusion = f32[32768]{0:T(1024)S(1)} fusion(f32[16,32768]{1,0:T(8,128)S(1)} %fusion.21, f32[96,16]{0,1:T(8,128)S(1)} %stack.69, f32[96,32768]{1,0:T(8,128)S(1)} %copy-done), kind=kOutput, calls=%fused_computation.2 | convolution fusion | flops 604995584 | bytes 14817280 | tf_op jit(solution)/shard_map/dot_general | solution.py:35
  389.1 1.7 copy.51
  390.8 0.7 multiply_bitcast_fusion
  (24 shorter events, 0.9 us)
Async XLA Ops:
  51.9 16.8 %copy-start.4 = (f32[1536,1,128]{2,1,0:T(1,128)S(1)}, f32[1536,1,128]{2,1,0:T(1,128)}, u32[]{:S(2)}) copy-start(f32[1536,1,128]{2,1,0:T(1,128)} %get-tuple-element.8) | copy-start | bytes 2359300
  51.9 17.7 %copy-start.3 = (f32[1536,1,128]{2,1,0:T(1,128)S(1)}, f32[1536,1,128]{2,1,0:T(1,128)}, u32[]{:S(2)}) copy-start(f32[1536,1,128]{2,1,0:T(1,128)} %get-tuple-element.7) | copy-start | bytes 2359300
  51.9 18.6 %copy-start.2 = (f32[1536,1,128]{2,1,0:T(1,128)S(1)}, f32[1536,1,128]{2,1,0:T(1,128)}, u32[]{:S(2)}) copy-start(f32[1536,1,128]{2,1,0:T(1,128)} %get-tuple-element.6) | copy-start | bytes 2359300
  51.9 19.6 %copy-start.1 = (f32[1536,1,128]{2,1,0:T(1,128)S(1)}, f32[1536,1,128]{2,1,0:T(1,128)}, u32[]{:S(2)}) copy-start(f32[1536,1,128]{2,1,0:T(1,128)} %get-tuple-element.5) | copy-start | bytes 2359300
  76.4 278.8 %all-to-all-start = ((f32[16,1536,1,128]{3,1,2,0:T(8,128)}), f32[16,1536,1,128]{3,1,2,0:T(8,128)}, u32[]{:S(2)}, u32[]{:S(2)}) async-start(f32[16,1536,1,128]{3,1,2,0:T(8,128)} %constant_dynamic-update-slice_fusion), calls=%async_computation | async-start | bytes 25165824 | tf_op jit(solution)/shard_map/all_to_all | solution.py:49
  368.9 8.2 %copy-start = (f32[96,32768]{1,0:T(8,128)S(1)}, f32[96,32768]{1,0:T(8,128)}, u32[]{:S(2)}) copy-start(f32[96,32768]{1,0:T(8,128)} %reshape_squeeze_reshape.3) | copy-start | bytes 37748740
